TPU v7x, 32 devices: a whole 2x2x4 slice. The times are simulated.
32 devices in a mesh: trial: 4 (over z), lat: 2 (over x), lon: 2 (over core), lev: 2 (over y).
Axes of the slice: x: 2, y: 2, z: 4, core: 2. Of those that a mesh axis runs over, the one named last changes fastest.
Arguments:
- density: float32 [32, 32, 256, 128], P(('trial', 'lat'), 'lon', 'lev'), parts along dimension 0, may hold values from 0.5 to 2
- crowding: float32 [32, 32, 256, 128], P(('trial', 'lat'), 'lon', 'lev'), parts along dimension 0, may hold values from 0.5 to 2
Outputs:
- scaled_field: float32 [32, 32, 256, 128], P(('trial', 'lat'), 'lon', 'lev'), parts along dimension 0
- density_end: float32 [32, 32, 256, 128], P(('trial', 'lat'), 'lon', 'lev'), parts along dimension 0
There are 4 independent parts, one for each index of `trial`. A program takes and returns all parts, laid end to end along the dimension named above; each array names one. Nothing has to cross between parts.
All inputs are finite; a program needn't handle non-finite values.
Results may differ from a plain program's by a relative error of at most 0.000058.
Values sent between devices are 32-bit elements; how exact they have to be, the bound alone decides.
A program may use at most 64 MiB of HBM per device.

v0:
```python
import jax
import jax.numpy as jnp
from jax import lax
from jax.sharding import PartitionSpec as P

STEPS = 4


def with_halo(cells, sides, width):
    for axis, dim in sides:
        count = lax.axis_size(axis)
        ends = count - 1
        head = lax.slice_in_dim(cells, 0, width, axis=dim)
        tail = lax.slice_in_dim(cells, cells.shape[dim] - width, cells.shape[dim], axis=dim)
        cells = jnp.concatenate(
            [
                lax.ppermute(tail, axis, [(i, (i + 1) % count) for i in range(ends)]),
                cells,
                lax.ppermute(head, axis, [((i + 1) % count, i) for i in range(ends)]),
            ],
            axis=dim,
        )
    return cells


def inner_cells(values, dims):
    for dim in dims:
        values = lax.slice_in_dim(values, 1, values.shape[dim] - 1, axis=dim)
    return values


def side_cells(values, dim, start, dims):
    others = [other for other in dims if other != dim]
    values = inner_cells(values, others)
    return lax.slice_in_dim(values, start, start + values.shape[dim] - 2, axis=dim)


def advance(padded, crowding):
    middle = inner_cells(padded, (0, 1, 2))
    lower = [side_cells(padded, dim, 0, (0, 1, 2)) for dim in (0, 1, 2)]
    upper = [side_cells(padded, dim, 2, (0, 1, 2)) for dim in (0, 1, 2)]
    spread = lower[0] + upper[0] + lower[1] + upper[1] + lower[2] + upper[2] - 6.0 * middle
    return middle + 0.1 * spread + 0.2 * middle * (1.0 - middle * crowding)


def shards(density, crowding):
    for step in range(STEPS):
        padded = with_halo(density, (("lat", 0), ("lon", 1), ("lev", 2)), 1)
        density = advance(padded, crowding)
    count = density.shape[1] * lax.axis_size("lon")
    guess = 1.0
    moved = density - guess
    totals, squares = lax.psum(
        (jnp.sum(moved, axis=1, keepdims=True), jnp.sum(moved * moved, axis=1, keepdims=True)),
        "lon",
    )
    line_mean = guess + totals / count
    centred = density - line_mean
    line_variance = squares / count - totals / count * (totals / count)
    scaled_field = centred * lax.rsqrt(line_variance + 0.0001)
    return (scaled_field, density)


def solution(mesh):
    placed = (P(("trial", "lat"), "lon", "lev", None), P(("trial", "lat"), "lon", "lev", None))
    return jax.shard_map(
        shards,
        mesh=mesh,
        in_specs=placed,
        out_specs=(
            P(("trial", "lat"), "lon", "lev", None),
            P(("trial", "lat"), "lon", "lev", None),
        ),
        check_vma=False,
    )
```

profile of v0, /device:TPU:0, one launch (start us, length us, event | category | flops | bytes accessed | tf_op | source)
XLA Modules:
  0.0 243.7 jit_solution(12184025480142498604)
XLA Ops:
  7.2 1.8 fusion.41
  9.1 5.1 %collective-permute-start = (f32[1,16,128,128]{3,2,1,0:T(8,128)S(1)}, f32[1,16,128,128]{3,2,1,0:T(8,128)S(1)}, u32[]{:S(2)}, u32[]{:S(2)}) collective-permute-start(f32[1,16,128,128]{3,2,1,0:T(8,128)S(1)} %get-tuple-element.30), channel_id=1, source_target_pairs={{0,4},{1,5},{2,6},{3,7},{8,12},{9,13},{10,14},{11,15},{16,20},{17,... | collective-permute-start | bytes 3145736 | tf_op jit(solution)/shard_map/ppermute | solution.py:17
  14.1 1.3 collective-permute-start.1
  15.4 21.0 %collective-permute-done = f32[1,16,128,128]{3,2,1,0:T(8,128)S(1)} collective-permute-done((f32[1,16,128,128]{3,2,1,0:T(8,128)S(1)}, f32[1,16,128,128]{3,2,1,0:T(8,128)S(1)}, u32[]{:S(2)}, u32[]{:S(2)}) %collective-permute-start) | collective-permute-done | bytes 1048608 | tf_op jit(solution)/shard_map/ppermute | solution.py:17
  36.5 0.1 constant_dynamic-update-slice_fusion.2
  36.6 0.5 constant_dynamic-update-slice_fusion.1
  37.1 3.6 %collective-permute-done.1 = f32[1,16,128,128]{3,2,1,0:T(8,128)S(1)} collective-permute-done((f32[1,16,128,128]{3,2,1,0:T(8,128)S(1)}, f32[1,16,128,128]{3,2,1,0:T(8,128)S(1)}, u32[]{:S(2)}, u32[]{:S(2)}) %collective-permute-start.1) | collective-permute-done | bytes 1048608 | tf_op jit(solution)/shard_map/ppermute | solution.py:19
  40.6 0.1 constant_dynamic-update-slice_fusion
  40.8 0.1 fusion.37
  40.8 1.6 collective-permute-start.2
  42.4 1.6 collective-permute-start.3
  44.0 2.3 collective-permute-done.3
  46.3 0.1 pad_maximum_fusion.90
  46.4 3.4 %collective-permute-start.4 = (f32[6,18,1,128]{3,2,1,0:T(1,128)S(1)}, f32[6,18,1,128]{3,2,1,0:T(1,128)S(1)}, u32[]{:S(2)}, u32[]{:S(2)}) collective-permute-start(f32[6,18,1,128]{3,2,1,0:T(1,128)S(1)} %get-tuple-element.13), channel_id=1, source_target_pairs={{0,1},{2,3},{4,5},{6,7},{8,9},{10,11},{12,13},{14,15},{16,17},{18,... | collective-permute-start | bytes 165896 | tf_op jit(solution)/shard_map/ppermute | solution.py:17
  49.8 1.3 collective-permute-start.5
  51.1 0.5 collective-permute-done.4
  51.6 4.3 %collective-permute-done.5 = f32[6,18,1,128]{3,2,1,0:T(1,128)S(1)} collective-permute-done((f32[6,18,1,128]{3,2,1,0:T(1,128)S(1)}, f32[6,18,1,128]{3,2,1,0:T(1,128)S(1)}, u32[]{:S(2)}, u32[]{:S(2)}) %collective-permute-start.5) | collective-permute-done | bytes 55328 | tf_op jit(solution)/shard_map/ppermute | solution.py:19
  55.9 9.8 %fusion.31 = f32[4,16,128,128]{3,2,1,0:T(8,128)S(1)} fusion(f32[4,16,128,128]{3,2,1,0:T(8,128)S(1)} %copy-done.2, f32[6,18,1,128]{3,2,1,0:T(1,128)S(1)} %collective-permute-done.5, f32[6,1,128,128]{3,2,1,0:T(8,128)S(1)} %collective-permute-done.3, f32[6,16,128,128]{3,2,1,0:T(8,128)} %copy-done.1, f32[6,1,128,128]{3,2,1,0:T(8,128)S(1)} %collective-permute-done.2, ...), kind=kLoop, calls=%fused_computation.86 | loop fusion | flops 25165824 | bytes 21868544 | tf_op jit(solution)/shard_map/add | solution.py:43
  65.6 0.2 fusion.40
  65.9 1.5 collective-permute-start.6
  67.4 1.3 collective-permute-start.7
  68.7 20.0 %collective-permute-done.6 = f32[1,16,128,128]{3,2,1,0:T(8,128)S(1)} collective-permute-done((f32[1,16,128,128]{3,2,1,0:T(8,128)S(1)}, f32[1,16,128,128]{3,2,1,0:T(8,128)S(1)}, u32[]{:S(2)}, u32[]{:S(2)}) %collective-permute-start.6) | collective-permute-done | bytes 1048608 | tf_op jit(solution)/shard_map/ppermute | solution.py:17
  88.7 4.2 %collective-permute-done.7 = f32[1,16,128,128]{3,2,1,0:T(8,128)S(1)} collective-permute-done((f32[1,16,128,128]{3,2,1,0:T(8,128)S(1)}, f32[1,16,128,128]{3,2,1,0:T(8,128)S(1)}, u32[]{:S(2)}, u32[]{:S(2)}) %collective-permute-start.7) | collective-permute-done | bytes 1048608 | tf_op jit(solution)/shard_map/ppermute | solution.py:19
  92.9 0.1 pad_maximum_fusion.72
  93.0 1.3 collective-permute-start.8
  94.3 1.3 collective-permute-start.9
  95.6 2.3 collective-permute-done.9
  97.9 0.1 pad_maximum_fusion.87
  98.0 1.9 collective-permute-start.10
  99.9 1.3 collective-permute-start.11
  101.2 0.5 collective-permute-done.10
  101.7 4.3 %collective-permute-done.11 = f32[6,18,1,128]{3,2,1,0:T(1,128)S(1)} collective-permute-done((f32[6,18,1,128]{3,2,1,0:T(1,128)S(1)}, f32[6,18,1,128]{3,2,1,0:T(1,128)S(1)}, u32[]{:S(2)}, u32[]{:S(2)}) %collective-permute-start.11) | collective-permute-done | bytes 55328 | tf_op jit(solution)/shard_map/ppermute | solution.py:19
  105.9 8.0 %fusion.22 = f32[4,16,128,128]{3,2,1,0:T(8,128)S(1)} fusion(f32[4,16,128,128]{3,2,1,0:T(8,128)S(1)} %fusion.31, f32[6,18,1,128]{3,2,1,0:T(1,128)S(1)} %collective-permute-done.11, f32[6,1,128,128]{3,2,1,0:T(8,128)S(1)} %collective-permute-done.9, f32[6,1,128,128]{3,2,1,0:T(8,128)S(1)} %collective-permute-done.8, ...), kind=kLoop, calls=%fused_computation.59 | loop fusion | flops 33554432 | bytes 15577088 | tf_op jit(solution)/shard_map/add | solution.py:43
  113.9 0.1 fusion.39
  114.0 1.5 collective-permute-start.12
  115.6 1.3 collective-permute-start.13
  116.9 20.0 %collective-permute-done.12 = f32[1,16,128,128]{3,2,1,0:T(8,128)S(1)} collective-permute-done((f32[1,16,128,128]{3,2,1,0:T(8,128)S(1)}, f32[1,16,128,128]{3,2,1,0:T(8,128)S(1)}, u32[]{:S(2)}, u32[]{:S(2)}) %collective-permute-start.12) | collective-permute-done | bytes 1048608 | tf_op jit(solution)/shard_map/ppermute | solution.py:17
  136.9 4.2 %collective-permute-done.13 = f32[1,16,128,128]{3,2,1,0:T(8,128)S(1)} collective-permute-done((f32[1,16,128,128]{3,2,1,0:T(8,128)S(1)}, f32[1,16,128,128]{3,2,1,0:T(8,128)S(1)}, u32[]{:S(2)}, u32[]{:S(2)}) %collective-permute-start.13) | collective-permute-done | bytes 1048608 | tf_op jit(solution)/shard_map/ppermute | solution.py:19
  141.1 1.3 collective-permute-start.14
  142.5 1.3 collective-permute-start.15
  143.8 2.3 collective-permute-done.15
  146.1 0.1 pad_maximum_fusion.82
  146.2 1.9 collective-permute-start.16
  148.0 1.3 collective-permute-start.17
  149.3 0.5 collective-permute-done.16
  149.8 4.3 %collective-permute-done.17 = f32[6,18,1,128]{3,2,1,0:T(1,128)S(1)} collective-permute-done((f32[6,18,1,128]{3,2,1,0:T(1,128)S(1)}, f32[6,18,1,128]{3,2,1,0:T(1,128)S(1)}, u32[]{:S(2)}, u32[]{:S(2)}) %collective-permute-start.17) | collective-permute-done | bytes 55328 | tf_op jit(solution)/shard_map/ppermute | solution.py:19
  154.1 8.0 %fusion.13 = f32[4,16,128,128]{3,2,1,0:T(8,128)S(1)} fusion(f32[4,16,128,128]{3,2,1,0:T(8,128)S(1)} %fusion.22, f32[6,18,1,128]{3,2,1,0:T(1,128)S(1)} %collective-permute-done.17, f32[6,1,128,128]{3,2,1,0:T(8,128)S(1)} %collective-permute-done.15, f32[6,1,128,128]{3,2,1,0:T(8,128)S(1)} %collective-permute-done.14, ...), kind=kLoop, calls=%fused_computation.32 | loop fusion | flops 33554432 | bytes 15577088 | tf_op jit(solution)/shard_map/add | solution.py:43
  162.1 0.2 fusion.38
  162.3 1.5 collective-permute-start.18
  163.8 1.3 collective-permute-start.19
  165.1 20.0 %collective-permute-done.18 = f32[1,16,128,128]{3,2,1,0:T(8,128)S(1)} collective-permute-done((f32[1,16,128,128]{3,2,1,0:T(8,128)S(1)}, f32[1,16,128,128]{3,2,1,0:T(8,128)S(1)}, u32[]{:S(2)}, u32[]{:S(2)}) %collective-permute-start.18) | collective-permute-done | bytes 1048608 | tf_op jit(solution)/shard_map/ppermute | solution.py:17
  185.1 4.2 %collective-permute-done.19 = f32[1,16,128,128]{3,2,1,0:T(8,128)S(1)} collective-permute-done((f32[1,16,128,128]{3,2,1,0:T(8,128)S(1)}, f32[1,16,128,128]{3,2,1,0:T(8,128)S(1)}, u32[]{:S(2)}, u32[]{:S(2)}) %collective-permute-start.19) | collective-permute-done | bytes 1048608 | tf_op jit(solution)/shard_map/ppermute | solution.py:19
  189.4 1.3 collective-permute-start.20
  190.7 1.3 collective-permute-start.21
  192.0 2.3 collective-permute-done.21
  194.3 0.1 pad_maximum_fusion.77
  194.4 1.9 collective-permute-start.22
  196.3 1.3 collective-permute-start.23
  197.6 0.5 collective-permute-done.22
  198.1 4.3 %collective-permute-done.23 = f32[6,18,1,128]{3,2,1,0:T(1,128)S(1)} collective-permute-done((f32[6,18,1,128]{3,2,1,0:T(1,128)S(1)}, f32[6,18,1,128]{3,2,1,0:T(1,128)S(1)}, u32[]{:S(2)}, u32[]{:S(2)}) %collective-permute-start.23) | collective-permute-done | bytes 55328 | tf_op jit(solution)/shard_map/ppermute | solution.py:19
  202.3 10.2 %add_reduce_fusion = (f32[4,128,128]{2,1,0:T(8,128)}, f32[4,128,128]{2,1,0:T(8,128)}, f32[4,16,128,128]{3,2,1,0:T(8,128)}) fusion(f32[4,16,128,128]{3,2,1,0:T(8,128)S(1)} %fusion.13, f32[4,16,128,128]{3,2,1,0:T(8,128)S(1)} %copy-done, f32[6,18,1,128]{3,2,1,0:T(1,128)S(1)} %collective-permute-done.23, f32[6,1,128,128]{3,2,1,0:T(8,128)S(1)} %collective-permute-done.21, ...), kind=kLoop, calls=%fused_computation.102 | loop fusion | flops 37617664 | bytes 16101376 | tf_op jit(solution)/shard_map/reduce_sum | solution.py:54
  212.6 18.2 %all-reduce.3.cloned.1.call-done = (f32[4,1,128,128]{3,2,0,1:T(8,128)}, f32[4,1,128,128]{3,2,0,1:T(8,128)}) async-done(((f32[4,1,128,128]{3,2,0,1:T(8,128)}, f32[4,1,128,128]{3,2,0,1:T(8,128)}), (f32[4,1,128,128]{3,2,0,1:T(8,128)}, f32[4,1,128,128]{3,2,0,1:T(8,128)})) %all-reduce.3.cloned.1.call-update) | async-done | bytes 524304 | tf_op jit(solution)/shard_map/psum | solution.py:53
  230.7 1.1 add_bitcast_fusion
  231.8 5.0 %subtract_multiply_fusion = f32[4,16,128,128]{3,2,1,0:T(8,128)} fusion(f32[4,16,128,128]{3,2,1,0:T(8,128)} %get-tuple-element.6, f32[4,128,128]{2,1,0:T(8,128)S(1)} %get-tuple-element.32, f32[4,128,128]{2,1,0:T(8,128)S(1)} %get-tuple-element.31), kind=kLoop, calls=%fused_computation.101 | loop fusion | flops 2097152 | bytes 8912896 | tf_op jit(solution)/shard_map/mul | solution.py:60
  (16 shorter events, 0.2 us)
Async XLA Ops:
  7.2 223.6 %all-reduce.3.cloned.1.call-start = ((), (), s32[]{:S(2)}) async-start(), calls=%async_computation | async-start | bytes 1048576 | tf_op jit(solution)/shard_map/psum | solution.py:53
  7.2 29.4 %copy-start.2 = (f32[4,16,128,128]{3,2,1,0:T(8,128)S(1)}, f32[4,16,128,128]{3,2,1,0:T(8,128)}, u32[]{:S(2)}) copy-start(f32[4,16,128,128]{3,2,1,0:T(8,128)} %param.2) | copy-start | bytes 12582916
  9.1 27.4 %collective-permute-start = (f32[1,16,128,128]{3,2,1,0:T(8,128)S(1)}, f32[1,16,128,128]{3,2,1,0:T(8,128)S(1)}, u32[]{:S(2)}, u32[]{:S(2)}) collective-permute-start(f32[1,16,128,128]{3,2,1,0:T(8,128)S(1)} %get-tuple-element.30), channel_id=1, source_target_pairs={{0,4},{1,5},{2,6},{3,7},{8,12},{9,13},{10,14},{11,15},{16,20},{17,... | collective-permute-start | bytes 3145736 | tf_op jit(solution)/shard_map/ppermute | solution.py:17
  14.1 26.5 %collective-permute-start.1 = (f32[1,16,128,128]{3,2,1,0:T(8,128)S(1)}, f32[1,16,128,128]{3,2,1,0:T(8,128)S(1)}, u32[]{:S(2)}, u32[]{:S(2)}) collective-permute-start(f32[1,16,128,128]{3,2,1,0:T(8,128)S(1)} %get-tuple-element.29), channel_id=1, source_target_pairs={{4,0},{5,1},{6,2},{7,3},{12,8},{13,9},{14,10},{15,11},{20,16},{21,... | collective-permute-start | bytes 3145736 | tf_op jit(solution)/shard_map/ppermute | solution.py:19
  40.6 5.7 %copy-start.3 = (f32[1,16,128,128]{3,2,1,0:T(8,128)}, f32[1,16,128,128]{3,2,1,0:T(8,128)S(1)}, u32[]{:S(2)}) copy-start(f32[1,16,128,128]{3,2,1,0:T(8,128)S(1)} %collective-permute-done.1) | copy-start | bytes 3145732
  40.7 5.6 %copy-start.1 = (f32[6,16,128,128]{3,2,1,0:T(8,128)}, f32[6,16,128,128]{3,2,1,0:T(8,128)S(1)}, u32[]{:S(2)}) copy-start(f32[6,16,128,128]{3,2,1,0:T(8,128)S(1)} %constant_dynamic-update-slice_fusion) | copy-start | bytes 18874372
  40.8 15.1 %copy-start = (f32[4,16,128,128]{3,2,1,0:T(8,128)S(1)}, f32[4,16,128,128]{3,2,1,0:T(8,128)}, u32[]{:S(2)}) copy-start(f32[4,16,128,128]{3,2,1,0:T(8,128)} %param.3) | copy-start | bytes 12582916
  40.8 3.2 %collective-permute-start.2 = (f32[6,1,128,128]{3,2,1,0:T(8,128)S(1)}, f32[6,1,128,128]{3,2,1,0:T(8,128)S(1)}, u32[]{:S(2)}, u32[]{:S(2)}) collective-permute-start(f32[6,1,128,128]{3,2,1,0:T(8,128)S(1)} %get-tuple-element.21), channel_id=1, source_target_pairs={{0,2},{1,3},{4,6},{5,7},{8,10},{9,11},{12,14},{13,15},{16,18},{17,... | collective-permute-start | bytes 1179656 | tf_op jit(solution)/shard_map/ppermute | solution.py:17
  42.4 3.9 %collective-permute-start.3 = (f32[6,1,128,128]{3,2,1,0:T(8,128)S(1)}, f32[6,1,128,128]{3,2,1,0:T(8,128)S(1)}, u32[]{:S(2)}, u32[]{:S(2)}) collective-permute-start(f32[6,1,128,128]{3,2,1,0:T(8,128)S(1)} %get-tuple-element.22), channel_id=1, source_target_pairs={{2,0},{3,1},{6,4},{7,5},{10,8},{11,9},{14,12},{15,13},{18,16},{19,... | collective-permute-start | bytes 1179656 | tf_op jit(solution)/shard_map/ppermute | solution.py:19
  46.4 5.2 %collective-permute-start.4 = (f32[6,18,1,128]{3,2,1,0:T(1,128)S(1)}, f32[6,18,1,128]{3,2,1,0:T(1,128)S(1)}, u32[]{:S(2)}, u32[]{:S(2)}) collective-permute-start(f32[6,18,1,128]{3,2,1,0:T(1,128)S(1)} %get-tuple-element.13), channel_id=1, source_target_pairs={{0,1},{2,3},{4,5},{6,7},{8,9},{10,11},{12,13},{14,15},{16,17},{18,... | collective-permute-start | bytes 165896 | tf_op jit(solution)/shard_map/ppermute | solution.py:17
  49.8 6.0 %collective-permute-start.5 = (f32[6,18,1,128]{3,2,1,0:T(1,128)S(1)}, f32[6,18,1,128]{3,2,1,0:T(1,128)S(1)}, u32[]{:S(2)}, u32[]{:S(2)}) collective-permute-start(f32[6,18,1,128]{3,2,1,0:T(1,128)S(1)} %get-tuple-element.14), channel_id=1, source_target_pairs={{1,0},{3,2},{5,4},{7,6},{9,8},{11,10},{13,12},{15,14},{17,16},{19,... | collective-permute-start | bytes 165896 | tf_op jit(solution)/shard_map/ppermute | solution.py:19
  65.9 22.8 %collective-permute-start.6 = (f32[1,16,128,128]{3,2,1,0:T(8,128)S(1)}, f32[1,16,128,128]{3,2,1,0:T(8,128)S(1)}, u32[]{:S(2)}, u32[]{:S(2)}) collective-permute-start(f32[1,16,128,128]{3,2,1,0:T(8,128)S(1)} %get-tuple-element.27), channel_id=1, source_target_pairs={{0,4},{1,5},{2,6},{3,7},{8,12},{9,13},{10,14},{11,15},{16,20},{17,... | collective-permute-start | bytes 3145736 | tf_op jit(solution)/shard_map/ppermute | solution.py:17
  67.4 25.5 %collective-permute-start.7 = (f32[1,16,128,128]{3,2,1,0:T(8,128)S(1)}, f32[1,16,128,128]{3,2,1,0:T(8,128)S(1)}, u32[]{:S(2)}, u32[]{:S(2)}) collective-permute-start(f32[1,16,128,128]{3,2,1,0:T(8,128)S(1)} %get-tuple-element.28), channel_id=1, source_target_pairs={{4,0},{5,1},{6,2},{7,3},{12,8},{13,9},{14,10},{15,11},{20,16},{21,... | collective-permute-start | bytes 3145736 | tf_op jit(solution)/shard_map/ppermute | solution.py:19
  93.0 2.6 %collective-permute-start.8 = (f32[6,1,128,128]{3,2,1,0:T(8,128)S(1)}, f32[6,1,128,128]{3,2,1,0:T(8,128)S(1)}, u32[]{:S(2)}, u32[]{:S(2)}) collective-permute-start(f32[6,1,128,128]{3,2,1,0:T(8,128)S(1)} %get-tuple-element.19), channel_id=1, source_target_pairs={{0,2},{1,3},{4,6},{5,7},{8,10},{9,11},{12,14},{13,15},{16,18},{17,... | collective-permute-start | bytes 1179656 | tf_op jit(solution)/shard_map/ppermute | solution.py:17
  94.3 3.6 %collective-permute-start.9 = (f32[6,1,128,128]{3,2,1,0:T(8,128)S(1)}, f32[6,1,128,128]{3,2,1,0:T(8,128)S(1)}, u32[]{:S(2)}, u32[]{:S(2)}) collective-permute-start(f32[6,1,128,128]{3,2,1,0:T(8,128)S(1)} %get-tuple-element.20), channel_id=1, source_target_pairs={{2,0},{3,1},{6,4},{7,5},{10,8},{11,9},{14,12},{15,13},{18,16},{19,... | collective-permute-start | bytes 1179656 | tf_op jit(solution)/shard_map/ppermute | solution.py:19
  98.0 3.7 %collective-permute-start.10 = (f32[6,18,1,128]{3,2,1,0:T(1,128)S(1)}, f32[6,18,1,128]{3,2,1,0:T(1,128)S(1)}, u32[]{:S(2)}, u32[]{:S(2)}) collective-permute-start(f32[6,18,1,128]{3,2,1,0:T(1,128)S(1)} %get-tuple-element.11), channel_id=1, source_target_pairs={{0,1},{2,3},{4,5},{6,7},{8,9},{10,11},{12,13},{14,15},{16,17},{18,... | collective-permute-start | bytes 165896 | tf_op jit(solution)/shard_map/ppermute | solution.py:17
  99.9 6.0 %collective-permute-start.11 = (f32[6,18,1,128]{3,2,1,0:T(1,128)S(1)}, f32[6,18,1,128]{3,2,1,0:T(1,128)S(1)}, u32[]{:S(2)}, u32[]{:S(2)}) collective-permute-start(f32[6,18,1,128]{3,2,1,0:T(1,128)S(1)} %get-tuple-element.12), channel_id=1, source_target_pairs={{1,0},{3,2},{5,4},{7,6},{9,8},{11,10},{13,12},{15,14},{17,16},{19,... | collective-permute-start | bytes 165896 | tf_op jit(solution)/shard_map/ppermute | solution.py:19
  114.0 22.8 %collective-permute-start.12 = (f32[1,16,128,128]{3,2,1,0:T(8,128)S(1)}, f32[1,16,128,128]{3,2,1,0:T(8,128)S(1)}, u32[]{:S(2)}, u32[]{:S(2)}) collective-permute-start(f32[1,16,128,128]{3,2,1,0:T(8,128)S(1)} %get-tuple-element.25), channel_id=1, source_target_pairs={{0,4},{1,5},{2,6},{3,7},{8,12},{9,13},{10,14},{11,15},{16,20},{17,... | collective-permute-start | bytes 3145736 | tf_op jit(solution)/shard_map/ppermute | solution.py:17
  115.6 25.5 %collective-permute-start.13 = (f32[1,16,128,128]{3,2,1,0:T(8,128)S(1)}, f32[1,16,128,128]{3,2,1,0:T(8,128)S(1)}, u32[]{:S(2)}, u32[]{:S(2)}) collective-permute-start(f32[1,16,128,128]{3,2,1,0:T(8,128)S(1)} %get-tuple-element.26), channel_id=1, source_target_pairs={{4,0},{5,1},{6,2},{7,3},{12,8},{13,9},{14,10},{15,11},{20,16},{21,... | collective-permute-start | bytes 3145736 | tf_op jit(solution)/shard_map/ppermute | solution.py:19
  141.1 2.6 %collective-permute-start.14 = (f32[6,1,128,128]{3,2,1,0:T(8,128)S(1)}, f32[6,1,128,128]{3,2,1,0:T(8,128)S(1)}, u32[]{:S(2)}, u32[]{:S(2)}) collective-permute-start(f32[6,1,128,128]{3,2,1,0:T(8,128)S(1)} %get-tuple-element.17), channel_id=1, source_target_pairs={{0,2},{1,3},{4,6},{5,7},{8,10},{9,11},{12,14},{13,15},{16,18},{17,... | collective-permute-start | bytes 1179656 | tf_op jit(solution)/shard_map/ppermute | solution.py:17
  142.5 3.6 %collective-permute-start.15 = (f32[6,1,128,128]{3,2,1,0:T(8,128)S(1)}, f32[6,1,128,128]{3,2,1,0:T(8,128)S(1)}, u32[]{:S(2)}, u32[]{:S(2)}) collective-permute-start(f32[6,1,128,128]{3,2,1,0:T(8,128)S(1)} %get-tuple-element.18), channel_id=1, source_target_pairs={{2,0},{3,1},{6,4},{7,5},{10,8},{11,9},{14,12},{15,13},{18,16},{19,... | collective-permute-start | bytes 1179656 | tf_op jit(solution)/shard_map/ppermute | solution.py:19
  146.2 3.7 %collective-permute-start.16 = (f32[6,18,1,128]{3,2,1,0:T(1,128)S(1)}, f32[6,18,1,128]{3,2,1,0:T(1,128)S(1)}, u32[]{:S(2)}, u32[]{:S(2)}) collective-permute-start(f32[6,18,1,128]{3,2,1,0:T(1,128)S(1)} %get-tuple-element.9), channel_id=1, source_target_pairs={{0,1},{2,3},{4,5},{6,7},{8,9},{10,11},{12,13},{14,15},{16,17},{18,... | collective-permute-start | bytes 165896 | tf_op jit(solution)/shard_map/ppermute | solution.py:17
  148.0 6.0 %collective-permute-start.17 = (f32[6,18,1,128]{3,2,1,0:T(1,128)S(1)}, f32[6,18,1,128]{3,2,1,0:T(1,128)S(1)}, u32[]{:S(2)}, u32[]{:S(2)}) collective-permute-start(f32[6,18,1,128]{3,2,1,0:T(1,128)S(1)} %get-tuple-element.10), channel_id=1, source_target_pairs={{1,0},{3,2},{5,4},{7,6},{9,8},{11,10},{13,12},{15,14},{17,16},{19,... | collective-permute-start | bytes 165896 | tf_op jit(solution)/shard_map/ppermute | solution.py:19
  162.3 22.8 %collective-permute-start.18 = (f32[1,16,128,128]{3,2,1,0:T(8,128)S(1)}, f32[1,16,128,128]{3,2,1,0:T(8,128)S(1)}, u32[]{:S(2)}, u32[]{:S(2)}) collective-permute-start(f32[1,16,128,128]{3,2,1,0:T(8,128)S(1)} %get-tuple-element.23), channel_id=1, source_target_pairs={{0,4},{1,5},{2,6},{3,7},{8,12},{9,13},{10,14},{11,15},{16,20},{17,... | collective-permute-start | bytes 3145736 | tf_op jit(solution)/shard_map/ppermute | solution.py:17
  163.8 25.5 %collective-permute-start.19 = (f32[1,16,128,128]{3,2,1,0:T(8,128)S(1)}, f32[1,16,128,128]{3,2,1,0:T(8,128)S(1)}, u32[]{:S(2)}, u32[]{:S(2)}) collective-permute-start(f32[1,16,128,128]{3,2,1,0:T(8,128)S(1)} %get-tuple-element.24), channel_id=1, source_target_pairs={{4,0},{5,1},{6,2},{7,3},{12,8},{13,9},{14,10},{15,11},{20,16},{21,... | collective-permute-start | bytes 3145736 | tf_op jit(solution)/shard_map/ppermute | solution.py:19
  189.4 2.6 %collective-permute-start.20 = (f32[6,1,128,128]{3,2,1,0:T(8,128)S(1)}, f32[6,1,128,128]{3,2,1,0:T(8,128)S(1)}, u32[]{:S(2)}, u32[]{:S(2)}) collective-permute-start(f32[6,1,128,128]{3,2,1,0:T(8,128)S(1)} %get-tuple-element.15), channel_id=1, source_target_pairs={{0,2},{1,3},{4,6},{5,7},{8,10},{9,11},{12,14},{13,15},{16,18},{17,... | collective-permute-start | bytes 1179656 | tf_op jit(solution)/shard_map/ppermute | solution.py:17
  190.7 3.6 %collective-permute-start.21 = (f32[6,1,128,128]{3,2,1,0:T(8,128)S(1)}, f32[6,1,128,128]{3,2,1,0:T(8,128)S(1)}, u32[]{:S(2)}, u32[]{:S(2)}) collective-permute-start(f32[6,1,128,128]{3,2,1,0:T(8,128)S(1)} %get-tuple-element.16), channel_id=1, source_target_pairs={{2,0},{3,1},{6,4},{7,5},{10,8},{11,9},{14,12},{15,13},{18,16},{19,... | collective-permute-start | bytes 1179656 | tf_op jit(solution)/shard_map/ppermute | solution.py:19
  194.4 3.7 %collective-permute-start.22 = (f32[6,18,1,128]{3,2,1,0:T(1,128)S(1)}, f32[6,18,1,128]{3,2,1,0:T(1,128)S(1)}, u32[]{:S(2)}, u32[]{:S(2)}) collective-permute-start(f32[6,18,1,128]{3,2,1,0:T(1,128)S(1)} %get-tuple-element.7), channel_id=1, source_target_pairs={{0,1},{2,3},{4,5},{6,7},{8,9},{10,11},{12,13},{14,15},{16,17},{18,... | collective-permute-start | bytes 165896 | tf_op jit(solution)/shard_map/ppermute | solution.py:17
  196.3 6.0 %collective-permute-start.23 = (f32[6,18,1,128]{3,2,1,0:T(1,128)S(1)}, f32[6,18,1,128]{3,2,1,0:T(1,128)S(1)}, u32[]{:S(2)}, u32[]{:S(2)}) collective-permute-start(f32[6,18,1,128]{3,2,1,0:T(1,128)S(1)} %get-tuple-element.8), channel_id=1, source_target_pairs={{1,0},{3,2},{5,4},{7,6},{9,8},{11,10},{13,12},{15,14},{17,16},{19,... | collective-permute-start | bytes 165896 | tf_op jit(solution)/shard_map/ppermute | solution.py:19
Sparse Core Ops, SparseCore 0:
  212.7 18.0 all-reduce.2
where the time goes:
time: 244 us
  waiting for transfers between devices  144 us (59%)
  other arithmetic  42.5 us (17%)
  starting transfers between devices  40 us (16%)
  between operations  14.4 us (6%)
  local copies, waits for them, and re-layouts  3.14 us (1%)
    ppermute x12, waiting for transfers between devices, with_halo(): lax.ppermute(tail, axis, [(i, (i + 1) % count) for i in range(ends)])  83.1 us
    ppermute x12, waiting for transfers between devices, with_halo(): lax.ppermute(head, axis, [((i + 1) % count, i) for i in range(ends)])  42.4 us
    add x3, other arithmetic, advance(): return middle + 0.1 * spread + 0.2 * middle * (1.0 - middle * crowding)  25.7 us
    ppermute x12, starting transfers between devices, with_halo(): lax.ppermute(tail, axis, [(i, (i + 1) % count) for i in range(ends)])  24.2 us
    psum x1, waiting for transfers between devices, shards(): lax.psum((jnp.sum(moved, axis=1, keepdims=True), jnp.sum(moved * moved, a...  18.2 us
    ppermute x12, starting transfers between devices, with_halo(): lax.ppermute(head, axis, [((i + 1) % count, i) for i in range(ends)])  15.8 us
    reduce_sum x1, other arithmetic, shards(): jnp.sum(moved, axis=1, keepdims=True)  10.2 us
    mul x1, other arithmetic, shards(): scaled_field = centred * lax.rsqrt(line_variance + 0.0001)  5.01 us
  transfers between devices with their start and end apart: 25, of which 21 were waited for; matrix products, arithmetic and copies ran while one was open for 0% of the time, Pallas kernels for 0%

commit v1 on v0

--- a/solution.py
+++ b/solution.py
@@ -1,9 +1,15 @@
+import functools
+
 import jax
 import jax.numpy as jnp
 from jax import lax
+from jax.experimental import pallas as pl
+from jax.experimental.pallas import tpu as pltpu
 from jax.sharding import PartitionSpec as P
 
 STEPS = 4
+PAD = 8
+MESH = pl.DeviceIdType.MESH
 
 
 def with_halo(cells, sides, width):
@@ -43,33 +49,315 @@
     return middle + 0.1 * spread + 0.2 * middle * (1.0 - middle * crowding)
 
 
-def shards(density, crowding):
+def general(density, crowding):
     for step in range(STEPS):
         padded = with_halo(density, (("lat", 0), ("lon", 1), ("lev", 2)), 1)
         density = advance(padded, crowding)
     count = density.shape[1] * lax.axis_size("lon")
-    guess = 1.0
-    moved = density - guess
+    moved = density - 1.0
     totals, squares = lax.psum(
         (jnp.sum(moved, axis=1, keepdims=True), jnp.sum(moved * moved, axis=1, keepdims=True)),
         "lon",
     )
-    line_mean = guess + totals / count
+    line_mean = 1.0 + totals / count
     centred = density - line_mean
     line_variance = squares / count - totals / count * (totals / count)
-    scaled_field = centred * lax.rsqrt(line_variance + 0.0001)
-    return (scaled_field, density)
+    return (centred * lax.rsqrt(line_variance + 0.0001), density)
+
+
+def tree_sum(terms):
+    terms = list(terms)
+    while len(terms) > 1:
+        terms = [sum(terms[i : i + 2][1:], terms[i]) for i in range(0, len(terms), 2)]
+    return terms[0]
+
+
+def kernel(lons, levs, parts, dens, crowd, out_scaled, out_dens,
+           field, cap, stats, peers, load_sem, face_send, face_recv,
+           lon_send, lon_recv, lev_send, lev_recv, stat_send, stat_recv):
+    rows, cols, deep, lanes = dens.shape
+    size = deep // parts
+    lat, lon, lev = lax.axis_index("lat"), lax.axis_index("lon"), lax.axis_index("lev")
+    has_left, has_right = lon > 0, lon < lons - 1
+    has_down, has_up = lev > 0, lev < levs - 1
+
+    def place(r):
+        return (1 - lat) * (rows - r) + lat * (r - 1)
+
+    loads = []
+    for r in range(1, rows + 1):
+        loads.append(pltpu.make_async_copy(
+            dens.at[place(r)],
+            field.at[0, r, pl.ds(1, cols), pl.ds(PAD, deep)],
+            load_sem.at[0, r - 1]))
+        loads.append(pltpu.make_async_copy(
+            crowd.at[place(r)], cap.at[r - 1], load_sem.at[1, r - 1]))
+    for copy in loads:
+        copy.start()
+
+    barrier = pltpu.get_barrier_semaphore()
+    pl.semaphore_signal(barrier, inc=1, device_id={"lat": 1 - lat}, device_id_type=MESH)
+    for j in range(1, lons):
+        pl.semaphore_signal(barrier, inc=1, device_id={"lon": lax.rem(lon + j, lons)}, device_id_type=MESH)
+    if levs > 1:
+        @pl.when(has_down)
+        def _():
+            pl.semaphore_signal(barrier, inc=1, device_id={"lev": lev - 1}, device_id_type=MESH)
+
+        @pl.when(has_up)
+        def _():
+            pl.semaphore_signal(barrier, inc=1, device_id={"lev": lev + 1}, device_id_type=MESH)
+    pl.semaphore_wait(barrier, lons + has_down.astype(jnp.int32) + has_up.astype(jnp.int32))
+
+    def face(t, k):
+        if t == 0:
+            src = dens.at[place(1), :, pl.ds(k * size, size)]
+        else:
+            src = field.at[t, 1, pl.ds(1, cols), pl.ds(PAD + k * size, size)]
+        return pltpu.make_async_remote_copy(
+            src_ref=src,
+            dst_ref=field.at[t, 0, pl.ds(1, cols), pl.ds(PAD + k * size, size)],
+            send_sem=face_send.at[t, k],
+            recv_sem=face_recv.at[t, k],
+            device_id={"lat": 1 - lat},
+            device_id_type=MESH,
+        )
+
+    def lon_side(t, right):
+        own, theirs = (cols, 0) if right else (1, cols + 1)
+        span = pl.ds(1, rows)
+        return pltpu.make_async_remote_copy(
+            src_ref=field.at[t, span, own, pl.ds(PAD, deep)],
+            dst_ref=field.at[t, span, theirs, pl.ds(PAD, deep)],
+            send_sem=lon_send.at[t, int(right)],
+            recv_sem=lon_recv.at[t, int(right)],
+            device_id={"lon": lon + 1 if right else lon - 1},
+            device_id_type=MESH,
+        )
+
+    def lev_side(t, up):
+        own, theirs = (PAD + deep - 1, PAD - 1) if up else (PAD, PAD + deep)
+        span = (pl.ds(1, rows), pl.ds(1, cols))
+        return pltpu.make_async_remote_copy(
+            src_ref=field.at[t, span[0], span[1], pl.ds(own, 1)],
+            dst_ref=field.at[t, span[0], span[1], pl.ds(theirs, 1)],
+            send_sem=lev_send.at[t, int(up)],
+            recv_sem=lev_recv.at[t, int(up)],
+            device_id={"lev": lev + 1 if up else lev - 1},
+            device_id_type=MESH,
+        )
+
+    def sides(t, act):
+        if lons > 1:
+            pl.when(has_right)(lambda: act(lon_side(t, True), 1))
+            pl.when(has_left)(lambda: act(lon_side(t, False), 0))
+        if levs > 1:
+            pl.when(has_up)(lambda: act(lev_side(t, True), 1))
+            pl.when(has_down)(lambda: act(lev_side(t, False), 0))
+
+    def start_sides(t):
+        sides(t, lambda copy, _: copy.start())
+
+    def wait_sides_sent(t):
+        sides(t, lambda copy, _: copy.wait_send())
+
+    def wait_sides(t):
+        if lons > 1:
+            pl.when(has_left)(lambda: lon_side(t, True).wait_recv())
+            pl.when(has_right)(lambda: lon_side(t, False).wait_recv())
+        if levs > 1:
+            pl.when(has_down)(lambda: lev_side(t, True).wait_recv())
+            pl.when(has_up)(lambda: lev_side(t, False).wait_recv())
+
+    def stat(part, j):
+        if part < parts:
+            pick = (0, slice(None), pl.ds(part * size, size))
+        else:
+            pick = (pl.ds(1, rows - 1),)
+        return pltpu.make_async_remote_copy(
+            src_ref=stats.at[pick],
+            dst_ref=peers.at[(j - 1,) + pick],
+            send_sem=stat_send.at[part, j - 1],
+            recv_sem=stat_recv.at[part, j - 1],
+            device_id={"lon": lax.rem(lon + j, lons)},
+            device_id_type=MESH,
+        )
+
+    for k in range(parts):
+        face(0, k).start()
+
+    def clear_cols(at):
+        for t in range(STEPS):
+            def row(i, _, t=t):
+                field[t, i, at, pl.ds(PAD, deep)] = jnp.zeros((deep, lanes), jnp.float32)
+                return 0
+            lax.fori_loop(1, rows + 1, row, 0)
+
+    def clear_level(at):
+        for t in range(STEPS):
+            def row(i, _, t=t):
+                def col(c, _):
+                    field[t, i, c, pl.ds(at, PAD)] = jnp.zeros((PAD, lanes), jnp.float32)
+                    return 0
+                return lax.fori_loop(1, cols + 1, col, 0)
+            lax.fori_loop(1, rows + 1, row, 0)
+
+    pl.when(jnp.logical_not(has_left))(lambda: clear_cols(0))
+    pl.when(jnp.logical_not(has_right))(lambda: clear_cols(cols + 1))
+    pl.when(jnp.logical_not(has_down))(lambda: clear_level(0))
+    pl.when(jnp.logical_not(has_up))(lambda: clear_level(PAD + deep))
+
+    for copy in loads:
+        copy.wait()
+    start_sides(0)
+
+    def cell(t, r, c, at, span, last):
+        here = field[t, r, c, pl.ds(PAD + at, span)]
+        near = (field[t, r, c - 1, pl.ds(PAD + at, span)] + field[t, r, c + 1, pl.ds(PAD + at, span)])
+        near += (field[t, r, c, pl.ds(PAD - 1 + at, span)] + field[t, r, c, pl.ds(PAD + 1 + at, span)])
+        near += field[t, r - 1, c, pl.ds(PAD + at, span)]
+        if not last:
+            near += field[t, r + 1, c, pl.ds(PAD + at, span)]
+        limit = cap[r - 1, c - 1, pl.ds(at, span)]
+        return here * (0.6 - 0.2 * (here * limit)) + 0.1 * near
+
+    def advance_row(t, r, at, span, last):
+        def col(c, _):
+            field[t + 1, r, c, pl.ds(PAD + at, span)] = cell(t, r, c, at, span, last)
+            return 0
+        lax.fori_loop(1, cols + 1, col, 0)
+
+    for t in range(STEPS - 1):
+        wait_sides(t)
+
+        def inner(r, _, t=t):
+            advance_row(t, r, 0, deep, False)
+            return 0
+
+        lax.fori_loop(2, rows, inner, 0)
+        advance_row(t, rows, 0, deep, True)
+        for k in range(parts):
+            face(t, k).wait_recv()
+            advance_row(t, 1, k * size, size, rows == 1)
+            face(t + 1, k).start()
+        start_sides(t + 1)
+
+    t = STEPS - 1
+    wait_sides(t)
+
+    def finish(r, at, last):
+        values = [cell(t, r, c, at, 8, last) for c in range(1, cols + 1)]
+        for c in range(cols):
+            out_dens[place(r), c, pl.ds(at, 8)] = values[c]
+        total = tree_sum(values)
+        mean = total * (1.0 / cols)
+        stats[r - 1, 0, pl.ds(at, 8)] = total
+        stats[r - 1, 1, pl.ds(at, 8)] = tree_sum([(v - mean) * (v - mean) for v in values])
+
+    def scale(r, at):
+        pair = [(stats[r - 1, 0, pl.ds(at, 8)], stats[r - 1, 1, pl.ds(at, 8)])]
+        for j in range(lons - 1):
+            pair.append((peers[j, r - 1, 0, pl.ds(at, 8)], peers[j, r - 1, 1, pl.ds(at, 8)]))
+        count = cols * lons
+        mean = tree_sum([p[0] for p in pair]) * (1.0 / count)
+        square = tree_sum([p[1] + cols * (p[0] * (1.0 / cols) - mean) ** 2 for p in pair])
+        gain = lax.rsqrt(square * (1.0 / count) + 0.0001)
+        for c in range(cols):
+            out_scaled[place(r), c, pl.ds(at, 8)] = (out_dens[place(r), c, pl.ds(at, 8)] - mean) * gain
+
+    def tiles(first, many, act):
+        def tile(i, _):
+            act(pl.multiple_of(i * 8, 8))
+            return 0
+        lax.fori_loop(first // 8, (first + many) // 8, tile, 0)
+
+    def each_inner(act):
+        def row(r, _):
+            tiles(0, deep, lambda at: act(r, at))
+            return 0
+        lax.fori_loop(2, rows, row, 0)
+
+    each_inner(lambda r, at: finish(r, at, False))
+    tiles(0, deep, lambda at: finish(rows, at, True))
+    for j in range(1, lons):
+        stat(parts, j).start()
+    for k in range(parts):
+        face(t, k).wait_recv()
+        tiles(k * size, size, lambda at: finish(1, at, False))
+        for j in range(1, lons):
+            stat(k, j).start()
+        if k == 0:
+            for j in range(1, lons):
+                stat(parts, j).wait_recv()
+            each_inner(scale)
+            tiles(0, deep, lambda at: scale(rows, at))
+        else:
+            for j in range(1, lons):
+                stat(k - 1, j).wait_recv()
+            tiles((k - 1) * size, size, lambda at: scale(1, at))
+    for s in range(STEPS):
+        for k in range(parts):
+            face(s, k).wait_send()
+        wait_sides_sent(s)
+    for j in range(1, lons):
+        stat(parts - 1, j).wait_recv()
+    tiles((parts - 1) * size, size, lambda at: scale(1, at))
+    for j in range(1, lons):
+        for part in range(parts + 1):
+            stat(part, j).wait_send()
+
+
+def one_kernel(lons, levs, density, crowding):
+    rows, cols, deep, lanes = density.shape
+    parts = 4
+    sem = pltpu.SemaphoreType.DMA
+    peers = max(lons - 1, 1)
+    out = pltpu.VMEM(density.shape, jnp.float32)
+    return pl.pallas_call(
+        functools.partial(kernel, lons, levs, parts),
+        out_shape=(out, out),
+        in_specs=[pl.BlockSpec(memory_space=pl.ANY)] * 2,
+        out_specs=[pl.BlockSpec(memory_space=pltpu.VMEM)] * 2,
+        scratch_shapes=[
+            pltpu.VMEM((STEPS, rows + 1, cols + 2, deep + 2 * PAD, lanes), jnp.float32),
+            pltpu.VMEM((rows, cols, deep, lanes), jnp.float32),
+            pltpu.VMEM((rows, 2, deep, lanes), jnp.float32),
+            pltpu.VMEM((peers, rows, 2, deep, lanes), jnp.float32),
+            sem((2, rows)),
+            sem((STEPS, parts)),
+            sem((STEPS, parts)),
+            sem((STEPS, 2)),
+            sem((STEPS, 2)),
+            sem((STEPS, 2)),
+            sem((STEPS, 2)),
+            sem((parts + 1, peers)),
+            sem((parts + 1, peers)),
+        ],
+        compiler_params=pltpu.CompilerParams(
+            collective_id=0, has_side_effects=True, vmem_limit_bytes=VMEM_LIMIT
+        ),
+    )(density, crowding)
+
+
+VMEM_LIMIT = 44 * 2**20
 
 
 def solution(mesh):
-    placed = (P(("trial", "lat"), "lon", "lev", None), P(("trial", "lat"), "lon", "lev", None))
+    lats, lons, levs = mesh.shape["lat"], mesh.shape["lon"], mesh.shape["lev"]
+
+    def shards(density, crowding):
+        rows, cols, deep, lanes = density.shape
+        words = lanes * (
+            STEPS * (rows + 1) * (cols + 2) * (deep + 2 * PAD)
+            + 3 * rows * cols * deep
+            + 2 * lons * rows * deep
+        )
+        fits = lats == 2 and rows > 1 and lanes == 128 and deep % 32 == 0 and 4 * words < VMEM_LIMIT
+        if fits:
+            return tuple(one_kernel(lons, levs, density, crowding))
+        return general(density, crowding)
+
+    spec = P(("trial", "lat"), "lon", "lev", None)
     return jax.shard_map(
-        shards,
-        mesh=mesh,
-        in_specs=placed,
-        out_specs=(
-            P(("trial", "lat"), "lon", "lev", None),
-            P(("trial", "lat"), "lon", "lev", None),
-        ),
-        check_vma=False,
+        shards, mesh=mesh, in_specs=(spec, spec), out_specs=(spec, spec), check_vma=False
     )

time: 244 us -> 102 us (0.42)
  waiting for transfers between devices: 144 us -> 0 us
  Pallas kernels: 0 us -> 96.8 us
  other arithmetic: 42.5 us -> 0 us
  starting transfers between devices: 40 us -> 0 us
  between operations: 14.4 us -> 0.64 us
    ppermute x24 -> x0, waiting for transfers between devices: 125 us -> none  [the longest x12 83.1 us: with_halo(): lax.ppermute(tail, axis, [(i, (i + 1) % count) for i in range(ends)])]
    pallas_call x0 -> x1, Pallas kernels: none -> 96.8 us  [one_kernel(): pl.pallas_call(functools.partial(kernel, lons, levs, parts), out_shape=(o...]
    ppermute x24 -> x0, starting transfers between devices: 40 us -> none  [the longest x12 24.2 us: with_halo(): lax.ppermute(tail, axis, [(i, (i + 1) % count) for i in range(ends)])]
    add x3 -> x0, other arithmetic: 25.7 us -> none  [advance(): return middle + 0.1 * spread + 0.2 * middle * (1.0 - middle * crowding)]
    psum x1 -> x0, waiting for transfers between devices: 18.2 us -> none  [shards(): lax.psum((jnp.sum(moved, axis=1, keepdims=True), jnp.sum(moved * moved, a...]
    reduce_sum x1 -> x0, other arithmetic: 10.2 us -> none  [shards(): jnp.sum(moved, axis=1, keepdims=True)]
    mul x1 -> x0, other arithmetic: 5.01 us -> none  [shards(): scaled_field = centred * lax.rsqrt(line_variance + 0.0001)]
    unnamed x10 -> x2, local copies, waits for them, and re-layouts: 0.6 us -> 4.03 us
  transfers between devices with their start and end apart: 25 -> 0, of which waited for: 21 -> 0; matrix products, arithmetic and copies ran while one was open for 0% -> 0% of each run, Pallas kernels for 0% -> 0%
where the time goes in v1:
time: 102 us; the launch traced here: 101 us
  Pallas kernels  96.8 us (95%)
  local copies, waits for them, and re-layouts  4.03 us (4%)
    pallas_call x1, Pallas kernels, one_kernel(): pl.pallas_call(functools.partial(kernel, lons, levs, parts), out_shape=(o...  96.8 us
    unnamed x2, local copies, waits for them, and re-layouts  4.03 us

profile of v1, /device:TPU:0, one launch (start us, length us, event | category | flops | bytes accessed | tf_op | source)
XLA Modules:
  0.0 101.5 jit_solution(11655630462149087919)
XLA Ops:
  0.6 96.8 %shard_map.41 = (f32[4,16,128,128]{3,2,1,0:T(8,128)S(1)}, f32[4,16,128,128]{3,2,1,0:T(8,128)S(1)}) custom-call(f32[4,16,128,128]{3,2,1,0:T(8,128)} %dens.1, f32[4,16,128,128]{3,2,1,0:T(8,128)} %crowd.1), custom_call_target="tpu_custom_call" | custom-call | tf_op jit(solution)/shard_map/pallas_call | solution.py:316
  97.5 2.0 %copy.6 = f32[4,16,128,128]{3,2,1,0:T(8,128)} copy(f32[4,16,128,128]{3,2,1,0:T(8,128)S(1)} %get-tuple-element.2) | data formatting | bytes 8388608
  99.5 2.0 %copy.7 = f32[4,16,128,128]{3,2,1,0:T(8,128)} copy(f32[4,16,128,128]{3,2,1,0:T(8,128)S(1)} %get-tuple-element.3) | data formatting | bytes 8388608

commit v2 on v1

--- a/solution.py
+++ b/solution.py
@@ -72,11 +72,11 @@
     return terms[0]
 
 
-def kernel(lons, levs, parts, dens, crowd, out_scaled, out_dens,
-           field, cap, stats, peers, load_sem, face_send, face_recv,
+def kernel(lons, levs, spans, dens, crowd, out_scaled, out_dens,
+           field, cap, stats, peers, load_sem, edge_sem, face_send, face_recv,
            lon_send, lon_recv, lev_send, lev_recv, stat_send, stat_recv):
     rows, cols, deep, lanes = dens.shape
-    size = deep // parts
+    parts = len(spans)
     lat, lon, lev = lax.axis_index("lat"), lax.axis_index("lon"), lax.axis_index("lev")
     has_left, has_right = lon > 0, lon < lons - 1
     has_down, has_up = lev > 0, lev < levs - 1
@@ -84,15 +84,23 @@
     def place(r):
         return (1 - lat) * (rows - r) + lat * (r - 1)
 
+    first = [
+        pltpu.make_async_copy(
+            dens.at[place(1), :, pl.ds(at, span)],
+            field.at[0, 1, pl.ds(1, cols), pl.ds(PAD + at, span)],
+            edge_sem.at[k])
+        for k, (at, span) in enumerate(spans)
+    ]
     loads = []
     for r in range(1, rows + 1):
-        loads.append(pltpu.make_async_copy(
-            dens.at[place(r)],
-            field.at[0, r, pl.ds(1, cols), pl.ds(PAD, deep)],
-            load_sem.at[0, r - 1]))
+        if r > 1:
+            loads.append(pltpu.make_async_copy(
+                dens.at[place(r)],
+                field.at[0, r, pl.ds(1, cols), pl.ds(PAD, deep)],
+                load_sem.at[0, r - 1]))
         loads.append(pltpu.make_async_copy(
             crowd.at[place(r)], cap.at[r - 1], load_sem.at[1, r - 1]))
-    for copy in loads:
+    for copy in first + loads:
         copy.start()
 
     barrier = pltpu.get_barrier_semaphore()
@@ -110,13 +118,10 @@
     pl.semaphore_wait(barrier, lons + has_down.astype(jnp.int32) + has_up.astype(jnp.int32))
 
     def face(t, k):
-        if t == 0:
-            src = dens.at[place(1), :, pl.ds(k * size, size)]
-        else:
-            src = field.at[t, 1, pl.ds(1, cols), pl.ds(PAD + k * size, size)]
+        at, span = spans[k]
         return pltpu.make_async_remote_copy(
-            src_ref=src,
-            dst_ref=field.at[t, 0, pl.ds(1, cols), pl.ds(PAD + k * size, size)],
+            src_ref=field.at[t, 1, pl.ds(1, cols), pl.ds(PAD + at, span)],
+            dst_ref=field.at[t, 0, pl.ds(1, cols), pl.ds(PAD + at, span)],
             send_sem=face_send.at[t, k],
             recv_sem=face_recv.at[t, k],
             device_id={"lat": 1 - lat},
@@ -171,7 +176,7 @@
 
     def stat(part, j):
         if part < parts:
-            pick = (0, slice(None), pl.ds(part * size, size))
+            pick = (0, slice(None), pl.ds(*spans[part]))
         else:
             pick = (pl.ds(1, rows - 1),)
         return pltpu.make_async_remote_copy(
@@ -184,6 +189,7 @@
         )
 
     for k in range(parts):
+        first[k].wait()
         face(0, k).start()
 
     def clear_cols(at):
@@ -238,7 +244,7 @@
         advance_row(t, rows, 0, deep, True)
         for k in range(parts):
             face(t, k).wait_recv()
-            advance_row(t, 1, k * size, size, rows == 1)
+            advance_row(t, 1, *spans[k], False)
             face(t + 1, k).start()
         start_sides(t + 1)
 
@@ -283,7 +289,7 @@
         stat(parts, j).start()
     for k in range(parts):
         face(t, k).wait_recv()
-        tiles(k * size, size, lambda at: finish(1, at, False))
+        tiles(*spans[k], lambda at: finish(1, at, False))
         for j in range(1, lons):
             stat(k, j).start()
         if k == 0:
@@ -294,27 +300,57 @@
         else:
             for j in range(1, lons):
                 stat(k - 1, j).wait_recv()
-            tiles((k - 1) * size, size, lambda at: scale(1, at))
+            tiles(*spans[k - 1], lambda at: scale(1, at))
     for s in range(STEPS):
         for k in range(parts):
             face(s, k).wait_send()
         wait_sides_sent(s)
     for j in range(1, lons):
         stat(parts - 1, j).wait_recv()
-    tiles((parts - 1) * size, size, lambda at: scale(1, at))
+    tiles(*spans[parts - 1], lambda at: scale(1, at))
     for j in range(1, lons):
         for part in range(parts + 1):
             stat(part, j).wait_send()
 
 
+def writer(scaled, dens, out_scaled, out_dens, sems):
+    copies = []
+    for i, (src, dst) in enumerate(((scaled, out_scaled), (dens, out_dens))):
+        for r in range(src.shape[0]):
+            copies.append(pltpu.make_async_copy(src.at[r], dst.at[r], sems.at[i, r]))
+    for copy in copies:
+        copy.start()
+    for copy in copies:
+        copy.wait()
+
+
+def written(scaled, dens):
+    out = jax.ShapeDtypeStruct(dens.shape, dens.dtype)
+    return pl.pallas_call(
+        writer,
+        out_shape=(out, out),
+        in_specs=[pl.BlockSpec(memory_space=pltpu.VMEM)] * 2,
+        out_specs=[pl.BlockSpec(memory_space=pl.ANY)] * 2,
+        scratch_shapes=[pltpu.SemaphoreType.DMA((2, dens.shape[0]))],
+        compiler_params=pltpu.CompilerParams(vmem_limit_bytes=2**20),
+    )(
+        pltpu.with_memory_space_constraint(scaled, pltpu.VMEM),
+        pltpu.with_memory_space_constraint(dens, pltpu.VMEM),
+    )
+
+
 def one_kernel(lons, levs, density, crowding):
     rows, cols, deep, lanes = density.shape
-    parts = 4
+    quarter = deep // 4
+    spans = [(k * quarter, quarter) for k in range(4)]
+    if quarter > 8:
+        spans[3:] = [(3 * quarter, quarter - 8), (deep - 8, 8)]
+    parts = len(spans)
     sem = pltpu.SemaphoreType.DMA
     peers = max(lons - 1, 1)
     out = pltpu.VMEM(density.shape, jnp.float32)
     return pl.pallas_call(
-        functools.partial(kernel, lons, levs, parts),
+        functools.partial(kernel, lons, levs, spans),
         out_shape=(out, out),
         in_specs=[pl.BlockSpec(memory_space=pl.ANY)] * 2,
         out_specs=[pl.BlockSpec(memory_space=pltpu.VMEM)] * 2,
@@ -324,6 +360,7 @@
             pltpu.VMEM((rows, 2, deep, lanes), jnp.float32),
             pltpu.VMEM((peers, rows, 2, deep, lanes), jnp.float32),
             sem((2, rows)),
+            sem((parts,)),
             sem((STEPS, parts)),
             sem((STEPS, parts)),
             sem((STEPS, 2)),
@@ -354,7 +391,7 @@
         )
         fits = lats == 2 and rows > 1 and lanes == 128 and deep % 32 == 0 and 4 * words < VMEM_LIMIT
         if fits:
-            return tuple(one_kernel(lons, levs, density, crowding))
+            return tuple(written(*one_kernel(lons, levs, density, crowding)))
         return general(density, crowding)
 
     spec = P(("trial", "lat"), "lon", "lev", None)

time: 102 us -> 101 us (level)
  local copies, waits for them, and re-layouts: 4.03 us -> 0 us
  Pallas kernels: 96.8 us -> 100 us
    unnamed x2 -> x0, local copies, waits for them, and re-layouts: 4.03 us -> none
    pallas_call x1 -> x2, Pallas kernels: 96.8 us -> 100 us  [the longest x1 96.6 us: one_kernel(): pl.pallas_call(functools.partial(kernel, lons, levs, spans), out_shape=(o...]
where the time goes in v2:
time: 101 us
  Pallas kernels  100 us (99%)
    pallas_call x1, Pallas kernels, one_kernel(): pl.pallas_call(functools.partial(kernel, lons, levs, spans), out_shape=(o...  96.6 us
    pallas_call x1, Pallas kernels, written(): pl.pallas_call(writer, out_shape=(out, out), in_specs=[pl.BlockSpec(memor...  3.37 us

profile of v2, /device:TPU:0, one launch (start us, length us, event | category | flops | bytes accessed | tf_op | source)
XLA Modules:
  0.0 100.6 jit_solution(4427001094056146887)
XLA Ops:
  0.6 96.6 %shard_map.41 = (f32[4,16,128,128]{3,2,1,0:T(8,128)S(1)}, f32[4,16,128,128]{3,2,1,0:T(8,128)S(1)}) custom-call(f32[4,16,128,128]{3,2,1,0:T(8,128)} %dens.1, f32[4,16,128,128]{3,2,1,0:T(8,128)} %crowd.1), custom_call_target="tpu_custom_call" | custom-call | tf_op jit(solution)/shard_map/pallas_call | solution.py:352
  97.2 3.4 %shard_map.42 = (f32[4,16,128,128]{3,2,1,0:T(8,128)}, f32[4,16,128,128]{3,2,1,0:T(8,128)}) custom-call(f32[4,16,128,128]{3,2,1,0:T(8,128)S(1)} %get-tuple-element.4.scaled, f32[4,16,128,128]{3,2,1,0:T(8,128)S(1)} %get-tuple-element.5.dens), custom_call_target="tpu_custom_call" | custom-call | tf_op jit(solution)/shard_map/pallas_call | solution.py:329

commit v3 on v2

--- a/solution.py
+++ b/solution.py
@@ -72,11 +72,11 @@
     return terms[0]
 
 
-def kernel(lons, levs, spans, dens, crowd, out_scaled, out_dens,
+def kernel(lons, levs, coarse, fine, dens, crowd, out_scaled, out_dens,
            field, cap, stats, peers, load_sem, edge_sem, face_send, face_recv,
            lon_send, lon_recv, lev_send, lev_recv, stat_send, stat_recv):
     rows, cols, deep, lanes = dens.shape
-    parts = len(spans)
+    spans, parts = fine, len(fine)
     lat, lon, lev = lax.axis_index("lat"), lax.axis_index("lon"), lax.axis_index("lev")
     has_left, has_right = lon > 0, lon < lons - 1
     has_down, has_up = lev > 0, lev < levs - 1
@@ -89,7 +89,7 @@
             dens.at[place(1), :, pl.ds(at, span)],
             field.at[0, 1, pl.ds(1, cols), pl.ds(PAD + at, span)],
             edge_sem.at[k])
-        for k, (at, span) in enumerate(spans)
+        for k, (at, span) in enumerate(coarse)
     ]
     loads = []
     for r in range(1, rows + 1):
@@ -117,8 +117,11 @@
             pl.semaphore_signal(barrier, inc=1, device_id={"lev": lev + 1}, device_id_type=MESH)
     pl.semaphore_wait(barrier, lons + has_down.astype(jnp.int32) + has_up.astype(jnp.int32))
 
+    def chunks(t):
+        return fine if t == STEPS - 1 else coarse
+
     def face(t, k):
-        at, span = spans[k]
+        at, span = chunks(t)[k]
         return pltpu.make_async_remote_copy(
             src_ref=field.at[t, 1, pl.ds(1, cols), pl.ds(PAD + at, span)],
             dst_ref=field.at[t, 0, pl.ds(1, cols), pl.ds(PAD + at, span)],
@@ -188,7 +191,7 @@
             device_id_type=MESH,
         )
 
-    for k in range(parts):
+    for k in range(len(coarse)):
         first[k].wait()
         face(0, k).start()
 
@@ -242,10 +245,12 @@
 
         lax.fori_loop(2, rows, inner, 0)
         advance_row(t, rows, 0, deep, True)
-        for k in range(parts):
+        for k in range(len(coarse)):
             face(t, k).wait_recv()
-            advance_row(t, 1, *spans[k], False)
-            face(t + 1, k).start()
+            advance_row(t, 1, *coarse[k], False)
+            for j, (at, _) in enumerate(chunks(t + 1)):
+                if coarse[k][0] <= at < sum(coarse[k]):
+                    face(t + 1, j).start()
         start_sides(t + 1)
 
     t = STEPS - 1
@@ -302,7 +307,7 @@
                 stat(k - 1, j).wait_recv()
             tiles(*spans[k - 1], lambda at: scale(1, at))
     for s in range(STEPS):
-        for k in range(parts):
+        for k in range(len(chunks(s))):
             face(s, k).wait_send()
         wait_sides_sent(s)
     for j in range(1, lons):
@@ -341,16 +346,15 @@
 
 def one_kernel(lons, levs, density, crowding):
     rows, cols, deep, lanes = density.shape
-    quarter = deep // 4
-    spans = [(k * quarter, quarter) for k in range(4)]
-    if quarter > 8:
-        spans[3:] = [(3 * quarter, quarter - 8), (deep - 8, 8)]
-    parts = len(spans)
+    half = deep // 2
+    coarse = [(0, half), (half, half)]
+    fine = coarse[:1] + [(half, half - 8), (deep - 8, 8)]
+    parts = len(fine)
     sem = pltpu.SemaphoreType.DMA
     peers = max(lons - 1, 1)
     out = pltpu.VMEM(density.shape, jnp.float32)
     return pl.pallas_call(
-        functools.partial(kernel, lons, levs, spans),
+        functools.partial(kernel, lons, levs, coarse, fine),
         out_shape=(out, out),
         in_specs=[pl.BlockSpec(memory_space=pl.ANY)] * 2,
         out_specs=[pl.BlockSpec(memory_space=pltpu.VMEM)] * 2,
@@ -360,7 +364,7 @@
             pltpu.VMEM((rows, 2, deep, lanes), jnp.float32),
             pltpu.VMEM((peers, rows, 2, deep, lanes), jnp.float32),
             sem((2, rows)),
-            sem((parts,)),
+            sem((len(coarse),)),
             sem((STEPS, parts)),
             sem((STEPS, parts)),
             sem((STEPS, 2)),

time: 101 us -> 101 us (level)
  no operation moved by 1% of the time
where the time goes in v3:
time: 101 us; the launch traced here: 100 us
  Pallas kernels  99.7 us (99%)
    pallas_call x1, Pallas kernels, one_kernel(): pl.pallas_call(functools.partial(kernel, lons, levs, coarse, fine), out_s...  96.4 us
    pallas_call x1, Pallas kernels, written(): pl.pallas_call(writer, out_shape=(out, out), in_specs=[pl.BlockSpec(memor...  3.37 us

profile of v3, /device:TPU:0, one launch (start us, length us, event | category | flops | bytes accessed | tf_op | source)
XLA Modules:
  0.0 100.4 jit_solution(10488187816553688914)
XLA Ops:
  0.6 96.4 %shard_map.41 = (f32[4,16,128,128]{3,2,1,0:T(8,128)S(1)}, f32[4,16,128,128]{3,2,1,0:T(8,128)S(1)}) custom-call(f32[4,16,128,128]{3,2,1,0:T(8,128)} %dens.1, f32[4,16,128,128]{3,2,1,0:T(8,128)} %crowd.1), custom_call_target="tpu_custom_call" | custom-call | tf_op jit(solution)/shard_map/pallas_call | solution.py:356
  97.0 3.4 %shard_map.42 = (f32[4,16,128,128]{3,2,1,0:T(8,128)}, f32[4,16,128,128]{3,2,1,0:T(8,128)}) custom-call(f32[4,16,128,128]{3,2,1,0:T(8,128)S(1)} %get-tuple-element.4.scaled, f32[4,16,128,128]{3,2,1,0:T(8,128)S(1)} %get-tuple-element.5.dens), custom_call_target="tpu_custom_call" | custom-call | tf_op jit(solution)/shard_map/pallas_call | solution.py:334

commit v4 on v3

--- a/solution.py
+++ b/solution.py
@@ -348,7 +348,7 @@
     rows, cols, deep, lanes = density.shape
     half = deep // 2
     coarse = [(0, half), (half, half)]
-    fine = coarse[:1] + [(half, half - 8), (deep - 8, 8)]
+    fine = coarse[:1] + [(half, half - 24), (deep - 24, 16), (deep - 8, 8)]
     parts = len(fine)
     sem = pltpu.SemaphoreType.DMA
     peers = max(lons - 1, 1)
@@ -393,7 +393,7 @@
             + 3 * rows * cols * deep
             + 2 * lons * rows * deep
         )
-        fits = lats == 2 and rows > 1 and lanes == 128 and deep % 32 == 0 and 4 * words < VMEM_LIMIT
+        fits = lats == 2 and rows > 1 and lanes == 128 and deep % 32 == 0 and deep >= 64 and 4 * words < VMEM_LIMIT
         if fits:
             return tuple(written(*one_kernel(lons, levs, density, crowding)))
         return general(density, crowding)

time: 101 us -> 101 us (level)
  no operation moved by 1% of the time
where the time goes in v4:
time: 101 us; the launch traced here: 100 us
  Pallas kernels  99.8 us (99%)
    pallas_call x1, Pallas kernels, one_kernel(): pl.pallas_call(functools.partial(kernel, lons, levs, coarse, fine), out_s...  96.5 us
    pallas_call x1, Pallas kernels, written(): pl.pallas_call(writer, out_shape=(out, out), in_specs=[pl.BlockSpec(memor...  3.37 us

profile of v4, /device:TPU:0, one launch (start us, length us, event | category | flops | bytes accessed | tf_op | source)
XLA Modules:
  0.0 100.5 jit_solution(18269321531009988518)
XLA Ops:
  0.6 96.5 %shard_map.41 = (f32[4,16,128,128]{3,2,1,0:T(8,128)S(1)}, f32[4,16,128,128]{3,2,1,0:T(8,128)S(1)}) custom-call(f32[4,16,128,128]{3,2,1,0:T(8,128)} %dens.1, f32[4,16,128,128]{3,2,1,0:T(8,128)} %crowd.1), custom_call_target="tpu_custom_call" | custom-call | tf_op jit(solution)/shard_map/pallas_call | solution.py:356
  97.1 3.4 %shard_map.42 = (f32[4,16,128,128]{3,2,1,0:T(8,128)}, f32[4,16,128,128]{3,2,1,0:T(8,128)}) custom-call(f32[4,16,128,128]{3,2,1,0:T(8,128)S(1)} %get-tuple-element.4.scaled, f32[4,16,128,128]{3,2,1,0:T(8,128)S(1)} %get-tuple-element.5.dens), custom_call_target="tpu_custom_call" | custom-call | tf_op jit(solution)/shard_map/pallas_call | solution.py:334
